TPU v7x, 32 devices: a whole 2x2x4 slice. The times are simulated.
32 devices in a mesh: groups: 2 (over y), seq: 4 (over z), heads: 2 (over x), cfg: 2 (over core).
Axes of the slice: x: 2, y: 2, z: 4, core: 2. Of those that a mesh axis runs over, the one named last changes fastest.
Arguments:
- video_tokens: bfloat16 [2, 8, 1152, 1024], P('cfg', ('groups', 'seq'), 'heads'), parts along dimension 1, may hold values from -6 to 6
- text_tokens: bfloat16 [2, 8, 1152, 128], P('cfg', ('groups', 'seq'), 'heads'), parts along dimension 1, may hold values from -6 to 6
- text_length: int32 [2, 8], P('cfg', ('groups', 'seq')), parts along dimension 1, may hold values from 1 to 128
- guide_numer: int32 [8], P(('groups', 'seq')), parts along dimension 0, may hold values from 2 to 8
- guide_denom: int32 [8], P(('groups', 'seq')), parts along dimension 0, may hold values from 4 to 8
- spatial_gain: bfloat16 [1152], replicated, may hold values from 0.25 to 1.75
- spatial_qkv: bfloat16 [3, 1152, 1152], P(None, 'heads'), may hold values from -0.11785113 to 0.11785113
- spatial_out: bfloat16 [1152, 1152], P('heads'), may hold values from -0.1875 to 0.1875
- temporal_gain: bfloat16 [1152], replicated, may hold values from 0.25 to 1.75
- temporal_qkv: bfloat16 [3, 1152, 1152], P(None, 'heads'), may hold values from -0.11785113 to 0.11785113
- temporal_out: bfloat16 [1152, 1152], P('heads'), may hold values from -0.1875 to 0.1875
Outputs:
- guided: bfloat16 [8, 1152, 1024], P(('groups', 'seq'), ('heads', 'cfg')), parts along dimension 0
There are 2 independent parts, one for each index of `groups`. A program takes and returns all parts, laid end to end along the dimension named above; an argument that names none is the same for every part. Nothing has to cross between parts.
Inputs may be any that keep to these rules, and one draw needn't show every extreme that they name: `text_length`: text tokens at or beyond a frame's length are padding.
All inputs are finite; a program needn't handle non-finite values.
Results may differ from a plain program's by a relative error of at most 0.009.
Values may be sent and summed in bfloat16 or wider, within the bound.
A program may use at most 64 MiB of HBM per device.

v0:
```python
import jax
import jax.numpy as jnp
from jax import lax
from jax.sharding import PartitionSpec as P

D = 1152
HEAD_DIM = 72
epsilon = 1e-06


def from_partner(shard, axis, stride):
    return lax.ppermute(shard, axis, [(i, i ^ 1 << stride) for i in range(lax.axis_size(axis))])


def softmax_along(scores, axis):
    top_score = jnp.max(scores, axis=axis, keepdims=True)
    expons = jnp.exp(scores - top_score)
    return (expons / jnp.sum(expons, axis=axis, keepdims=True)).astype(jnp.bfloat16)


def project_piece(piece, gain_vector, weights, parts):
    gain_piece = gain_vector.astype(jnp.float32)
    weight_piece = weights[parts]
    piece_wide = piece.astype(jnp.float32)
    scaled = (piece_wide * gain_piece[None, :, None]).astype(jnp.bfloat16)
    product = jnp.einsum("kod,fdp->fkop", weight_piece, scaled, preferred_element_type=jnp.float32)
    return (product, jnp.sum(piece_wide * piece_wide, axis=1))


def add_mixed(piece, matrix):
    return jnp.einsum("oc,fcp->fop", matrix, piece, preferred_element_type=jnp.float32)


def shards(
    video_tokens,
    text_tokens,
    text_length,
    guide_numer,
    guide_denom,
    spatial_gain,
    spatial_qkv,
    spatial_out,
    temporal_gain,
    temporal_qkv,
    temporal_out,
):
    frame_count = video_tokens.shape[1]
    width = video_tokens.shape[2]
    positions = video_tokens.shape[3]
    text_count = text_tokens.shape[3]
    local_heads = width // HEAD_DIM
    frame_tokens = video_tokens[0]
    frame_text = text_tokens[0]
    video_piece = lax.all_gather(frame_tokens, "heads", axis=1, tiled=True)
    text_piece = lax.all_gather(frame_text, "heads", axis=1, tiled=True)
    video_add, video_sq = project_piece(video_piece, spatial_gain, spatial_qkv, slice(0, 3))
    text_add, text_sq = project_piece(text_piece, spatial_gain, spatial_qkv, slice(1, 3))
    mixed = (video_add * lax.rsqrt(video_sq / D + epsilon)[:, None, None, :]).astype(jnp.bfloat16)
    mixed = mixed.reshape(frame_count, 3, local_heads, HEAD_DIM, positions)
    context = (text_add * lax.rsqrt(text_sq / D + epsilon)[:, None, None, :]).astype(jnp.bfloat16)
    context = context.reshape(frame_count, 2, local_heads, HEAD_DIM, text_count)
    key_rows = jnp.concatenate([mixed[:, 1], context[:, 0]], axis=3)
    value_rows = jnp.concatenate([mixed[:, 2], context[:, 1]], axis=3)
    query_all = mixed[:, 0]
    text_valid = jnp.arange(text_count, dtype=jnp.int32)[None, :] < text_length[0][:, None]
    valid_keys = jnp.concatenate(
        [jnp.ones((frame_count, positions), dtype=bool), text_valid], axis=1
    )
    block_rows = min(512, positions)
    block_count = positions // block_rows
    frame_ids = jnp.repeat(jnp.arange(frame_count, dtype=jnp.int32), block_count)
    block_ids = jnp.tile(jnp.arange(block_count, dtype=jnp.int32), frame_count)

    def block_step(inputs):
        frame_id, block_id = inputs
        query_rows = lax.dynamic_slice_in_dim(
            query_all[frame_id], block_id * block_rows, block_rows, 2
        )
        scores = jnp.einsum(
            "hep,hek->hpk", query_rows, key_rows[frame_id], preferred_element_type=jnp.float32
        )
        scores = scores * HEAD_DIM ** (-0.5)
        scores = jnp.where(valid_keys[frame_id][None, None, :], scores, -jnp.inf)
        weights = softmax_along(scores, 2)
        result = jnp.einsum(
            "hpk,hek->hep", weights, value_rows[frame_id], preferred_element_type=jnp.float32
        )
        return result.astype(jnp.bfloat16)

    attended = lax.map(block_step, (frame_ids, block_ids))
    attended = attended.reshape(frame_count, block_count, local_heads, HEAD_DIM, block_rows)
    attended = jnp.transpose(attended, (0, 2, 3, 1, 4)).reshape(frame_count, width, positions)
    update = add_mixed(lax.all_gather(attended, "heads", axis=1, tiled=True), spatial_out)
    after_spatial = (frame_tokens.astype(jnp.float32) + update).astype(jnp.bfloat16)
    own_rows = lax.all_to_all(after_spatial, "seq", split_axis=2, concat_axis=0, tiled=True)
    frames_all = own_rows.shape[0]
    columns = own_rows.shape[2]
    piece_add, piece_sq = project_piece(
        lax.all_gather(own_rows, "heads", axis=1, tiled=True),
        temporal_gain,
        temporal_qkv,
        slice(0, 3),
    )
    mixed_time = (piece_add * lax.rsqrt(piece_sq / D + epsilon)[:, None, None, :]).astype(
        jnp.bfloat16
    )
    mixed_time = mixed_time.reshape(frames_all, 3, local_heads, HEAD_DIM, columns)
    time_scores = jnp.einsum(
        "fhep,ghep->hfgp", mixed_time[:, 0], mixed_time[:, 1], preferred_element_type=jnp.float32
    )
    time_weights = softmax_along(time_scores * HEAD_DIM ** (-0.5), 2)
    attended_time = jnp.einsum(
        "hfgp,ghep->fhep", time_weights, mixed_time[:, 2], preferred_element_type=jnp.float32
    )
    attended_time = attended_time.astype(jnp.bfloat16).reshape(frames_all, width, columns)
    update_time = add_mixed(
        lax.all_gather(attended_time, "heads", axis=1, tiled=True), temporal_out
    )
    block_out = (own_rows.astype(jnp.float32) + update_time).astype(jnp.bfloat16)
    returned = lax.all_to_all(block_out, "seq", split_axis=0, concat_axis=2, tiled=True)
    half_width = width // 2
    partner = from_partner(returned, "cfg", 0)
    branch_index = lax.axis_index("cfg")
    cond_full = jnp.where(branch_index == 0, returned, partner)
    uncond_full = jnp.where(branch_index == 0, partner, returned)
    cond_part = lax.dynamic_slice_in_dim(cond_full, branch_index * half_width, half_width, 1)
    uncond_part = lax.dynamic_slice_in_dim(uncond_full, branch_index * half_width, half_width, 1)
    ratio = guide_numer.astype(jnp.float32) / guide_denom.astype(jnp.float32)
    cond_wide = cond_part.astype(jnp.float32)
    uncond_wide = uncond_part.astype(jnp.float32)
    return (uncond_wide + ratio[:, None, None] * (cond_wide - uncond_wide)).astype(jnp.bfloat16)


def solution(mesh):
    return jax.shard_map(
        shards,
        mesh=mesh,
        in_specs=(
            P("cfg", ("groups", "seq"), "heads", None),
            P("cfg", ("groups", "seq"), "heads", None),
            P("cfg", ("groups", "seq")),
            P(("groups", "seq")),
            P(("groups", "seq")),
            P(),
            P(None, "heads", None),
            P("heads", None),
            P(),
            P(None, "heads", None),
            P("heads", None),
        ),
        out_specs=P(("groups", "seq"), ("heads", "cfg"), None),
        check_vma=False,
    )
```

profile of v0, /device:TPU:0, one launch (start us, length us, event | category | flops | bytes accessed | tf_op | source)
XLA Modules:
  0.0 359.0 jit_solution(843548291912899709)
XLA Ops:
  6.5 0.0 copy-start
  6.5 0.0 all-gather.12.cloned.1.call-start
  6.5 0.7 all-gather.12.cloned.1.call-update
  7.3 0.0 all-gather.8.cloned.1.call-start
  7.3 0.7 convert_element_type.98
  8.7 7.7 %all-gather.1 = bf16[1,1,1152,128]{3,2,1,0:T(8,128)(2,1)S(1)} all-gather(bf16[1,1,576,128]{3,2,1,0:T(8,128)(2,1)} %param.14), channel_id=3, replica_groups=mesh['groups'=2,'seq'=4,'heads'=2,'cfg'=2] {'heads'}, dimensions={2}, use_global_device_ids=true | all-gather | bytes 442368 | tf_op jit(solution)/shard_map/all_gather | solution.py:55
  16.4 0.2 fusion.93
  16.6 3.0 fusion.87
  19.6 28.1 %all-gather.12.cloned.1.call-done = bf16[1,1,1152,1024]{3,2,1,0:T(8,128)(2,1)} async-done(((bf16[1,1,576,1024]{3,2,1,0:T(8,128)(2,1)}), bf16[1,1,1152,1024]{3,2,1,0:T(8,128)(2,1)}) %all-gather.12.cloned.1.call-update) | async-done | bytes 2359312 | tf_op jit(solution)/shard_map/all_gather | solution.py:54
  47.7 2.3 fusion.50
  50.0 0.0 copy-done.3
  50.1 7.3 %fusion.48 = bf16[1,1024,3,576]{1,3,2,0:T(8,128)(2,1)S(1)} fusion(f32[1024]{0:T(1024)S(1)} %add_rsqrt_fusion.1, bf16[3,576,1152]{2,1,0:T(8,128)(2,1)} %param.19, bf16[1,1,1152,1024]{3,2,1,0:T(8,128)(2,1)S(1)} %copy-done.3, f32[1152]{0:T(1024)S(1)} %convert_element_type.98), kind=kOutput, calls=%fused_computation.28 | convolution fusion | flops 4083941376 | bytes 9888256 | tf_op jit(solution)/shard_map/kod,fdp->fkop/dot_general | solution.py:26
  57.3 1.4 slice_bitcast_fusion
  58.7 1.3 pad_maximum_fusion
  60.1 37.0 %while.10 = (s32[]{:T(128)}, bf16[2,8,72,512]{3,2,1,0:T(8,128)(2,1)}, pred[1,1152]{1,0:T(4,128)(4,1)S(1)}, s32[2]{0:T(128)S(1)}, bf16[1,8,72,1024]{3,2,1,0:T(8,1...) while((s32[]{:T(128)}, ...), condition=%wide.region_5.6_spmd, body=%wide.region_2.5_spmd.sunk | while | flops 2081200384 | bytes 5788856 | solution.py:90
  60.5 0.7 dynamic_slice.50
  61.9 7.0 %exponential_reduce_fusion.2 = f32[8,512]{1,0:T(8,128)S(1)} fusion(pred[1152]{0:T(1024)(128)(4,1)S(1)} %reduce.5, bf16[1,8,72,1152]{3,2,1,0:T(8,128)(2,1)S(1)} %get-tuple-element.139, bf16[1,8,72,1024]{3,2,1,0:T(8,128)(2,1)} %get-tuple-element.138, s32[]{:T(128)S(6)} %select_n.52), kind=kOutput, calls=%fused_computation.5.clone.1 | convolution fusion | flops 698352768 | bytes 1934468 | tf_op jit(solution)/shard_map/while/body/eval_jaxpr/sub | solution.py:17
  69.0 9.8 %fusion.120 = bf16[2,8,72,512]{3,2,1,0:T(8,128)(2,1)} fusion(bf16[2,8,72,512]{3,2,1,0:T(8,128)(2,1)} %get-tuple-element.123, s32[]{:T(128)} %get-tuple-element.122, bf16[1,8,72,1152]{3,2,1,0:T(8,128)(2,1)} %get-tuple-element.140, f32[8,512]{1,0:T(8,128)S(1)} %exponential_reduce_fusion.2, pred[1152]{0:T(1024)(128)(4,1)S(1)} %reduce.5, ...), kind=kOutput, calls=%fused_computation.13.clone.1 | convolution fusion | flops 1382847616 | bytes 3851908 | tf_op jit(solution)/shard_map/while/body/eval_jaxpr/hpk,hek->hep/dot_general | solution.py:85
  78.8 0.7 dynamic_slice.50
  80.2 7.0 %exponential_reduce_fusion.2 = f32[8,512]{1,0:T(8,128)S(1)} fusion(pred[1152]{0:T(1024)(128)(4,1)S(1)} %reduce.5, bf16[1,8,72,1152]{3,2,1,0:T(8,128)(2,1)S(1)} %get-tuple-element.139, bf16[1,8,72,1024]{3,2,1,0:T(8,128)(2,1)} %get-tuple-element.138, s32[]{:T(128)S(6)} %select_n.52), kind=kOutput, calls=%fused_computation.5.clone.1 | convolution fusion | flops 698352768 | bytes 1934468 | tf_op jit(solution)/shard_map/while/body/eval_jaxpr/sub | solution.py:17
  87.2 9.8 %fusion.120 = bf16[2,8,72,512]{3,2,1,0:T(8,128)(2,1)} fusion(bf16[2,8,72,512]{3,2,1,0:T(8,128)(2,1)} %get-tuple-element.123, s32[]{:T(128)} %get-tuple-element.122, bf16[1,8,72,1152]{3,2,1,0:T(8,128)(2,1)} %get-tuple-element.140, f32[8,512]{1,0:T(8,128)S(1)} %exponential_reduce_fusion.2, pred[1152]{0:T(1024)(128)(4,1)S(1)} %reduce.5, ...), kind=kOutput, calls=%fused_computation.13.clone.1 | convolution fusion | flops 1382847616 | bytes 3851908 | tf_op jit(solution)/shard_map/while/body/eval_jaxpr/hpk,hek->hep/dot_general | solution.py:85
  97.1 2.5 copy.43
  99.6 1.7 reshape.105
  101.2 0.0 all-gather.8.cloned.1.call-update
  101.3 0.2 all-gather.14.cloned.1.call-start
  101.5 36.0 %all-gather.8.cloned.1.call-done = bf16[1,1152,1024]{2,1,0:T(8,128)(2,1)} async-done(((bf16[1,576,1024]{2,1,0:T(8,128)(2,1)}), bf16[1,1152,1024]{2,1,0:T(8,128)(2,1)}) %all-gather.8.cloned.1.call-update) | async-done | bytes 2359312 | tf_op jit(solution)/shard_map/all_gather | solution.py:93
  137.5 0.0 copy-done
  137.5 3.7 %fusion.64 = bf16[1,576,1024]{2,1,0:T(8,128)(2,1)S(1)} fusion(bf16[576,1152]{1,0:T(8,128)(2,1)S(1)} %copy-done, bf16[1,1152,1024]{2,1,0:T(8,128)(2,1)} %all-gather.8.cloned.1.call-done, bf16[1,1,576,1024]{3,2,1,0:T(8,128)(2,1)} %param.13), kind=kOutput, calls=%fused_computation.47 | convolution fusion | flops 1360723968 | bytes 6045696 | tf_op jit(solution)/shard_map/oc,fcp->fop/dot_general | solution.py:31
  141.1 4.1 %copy.44 = bf16[1,576,1024]{1,0,2:T(2,128)(2,1)} copy(bf16[1,576,1024]{2,1,0:T(8,128)(2,1)S(1)} %fusion.64) | data formatting | bytes 2359296 | tf_op jit(solution)/shard_map/convert_element_type | solution.py:94
  145.3 0.5 broadcast.82
  145.8 9.9 %reduce.3 = bf16[1024,576]{1,0:T(8,128)(2,1)S(1)} reduce(bf16[1024,1,576]{2,1,0:T(2,128)(2,1)} %bitcast.189, bf16[]{:T(256)} %broadcast.82), dimensions={1}, to_apply=%bitcast.164.reduce_sub_computation | reduce | bytes 2359298
  155.7 2.6 reshape.124
  158.3 33.0 %all_to_all.36 = bf16[4,2,73728]{2,1,0:T(2,128)(2,1)S(1)} all-to-all(bf16[4,2,73728]{2,1,0:T(2,128)(2,1)} %reshape.124), channel_id=1, replica_groups=mesh['groups'=2,'seq'=4,'heads'=2,'cfg'=2] {'seq'}, dimensions={0} | all-to-all | bytes 2359296 | tf_op jit(solution)/shard_map/all_to_all | solution.py:95
  191.3 3.3 reshape.125
  194.5 1.9 copy.57
  196.5 0.0 copy-start.5
  196.5 1.5 copy.46
  197.9 0.0 all-gather.14.cloned.1.call-update
  198.0 0.3 all-gather.10.cloned.1.call-start
  198.2 0.0 copy-done.5
  198.3 34.1 %all-gather.14.cloned.1.call-done = bf16[4,1,1152,256]{3,2,0,1:T(8,128)(2,1)} async-done(((bf16[4,1,576,256]{3,2,0,1:T(8,128)(2,1)}), bf16[4,1,1152,256]{3,2,0,1:T(8,128)(2,1)}) %all-gather.14.cloned.1.call-update) | async-done | bytes 2359312 | tf_op jit(solution)/shard_map/all_gather | solution.py:99
  232.3 2.3 fusion.52
  234.6 0.1 copy-done.4
  234.7 7.2 %multiply_convert_fusion = bf16[4,256,3,576]{1,3,2,0:T(8,128)(2,1)S(1)} fusion(f32[4,256]{1,0:T(4,128)S(1)} %add_rsqrt_fusion, bf16[3,576,1152]{2,1,0:T(8,128)(2,1)} %param.22, bf16[4,1,1152,256]{3,2,0,1:T(8,128)(2,1)S(1)} %copy-done.4, f32[1152]{0:T(1024)S(1)} %convert_element_type.109), kind=kOutput, calls=%fused_computation.29 | convolution fusion | flops 4083941376 | bytes 9888256 | tf_op jit(solution)/shard_map/kod,fdp->fkop/dot_general | solution.py:26
  241.9 1.9 fusion.104
  243.8 2.8 copy.59
  246.7 4.1 %copy.60 = bf16[4,1,8,72,256]{3,0,4,2,1:T(4,128)(2,1)} copy(bf16[4,1,8,72,256]{4,3,2,1,0:T(8,128)(2,1)} %get-tuple-element.59) | data formatting | bytes 2359296
  250.7 5.8 %fusion.71 = f32[8,256,4,4]{3,2,1,0:T(4,128)} fusion(bf16[4,1,8,72,256]{3,0,4,2,1:T(4,128)(2,1)} %copy.60, bf16[4,1,8,72,256]{3,0,4,2,1:T(4,128)(2,1)S(1)} %copy.59), kind=kOutput, calls=%fused_computation.54 | convolution fusion | flops 4718592 | bytes 2490368 | tf_op jit(solution)/shard_map/fhep,ghep->hfgp/dot_general | solution.py:108
  256.5 2.8 copy.50
  259.4 0.0 copy-start.1
  259.5 2.1 copy.51
  261.6 0.0 copy-done.1
  261.6 2.5 copy.58
  264.1 5.8 %convert_bitcast_fusion = bf16[4,8,72,256]{2,0,3,1:T(4,128)(2,1)} fusion(bf16[8,4,4,256]{2,1,3,0:T(4,128)(2,1)} %copy.51, bf16[4,1,8,72,256]{3,0,4,2,1:T(4,128)(2,1)} %copy.58), kind=kOutput, calls=%fused_computation.59 | convolution fusion | flops 5308416 | bytes 2424832 | tf_op jit(solution)/shard_map/hfgp,ghep->fhep/dot_general | solution.py:112
  269.9 4.2 %copy.52 = bf16[4,8,72,256]{3,2,1,0:T(8,128)(2,1)} copy(bf16[4,8,72,256]{2,0,3,1:T(4,128)(2,1)} %convert_bitcast_fusion) | data formatting | bytes 2359296 | tf_op jit(solution)/shard_map/convert_element_type | solution.py:115
  274.1 0.0 all-gather.10.cloned.1.call-update
  274.1 36.2 %all-gather.10.cloned.1.call-done = bf16[4,1152,256]{2,1,0:T(8,128)(2,1)} async-done(((bf16[4,576,256]{2,1,0:T(8,128)(2,1)}), bf16[4,1152,256]{2,1,0:T(8,128)(2,1)}) %all-gather.10.cloned.1.call-update) | async-done | bytes 2359312 | tf_op jit(solution)/shard_map/all_gather | solution.py:117
  310.3 0.0 copy-done.2
  310.3 3.8 %fusion.63 = bf16[4,576,256]{2,1,0:T(8,128)(2,1)S(1)} fusion(bf16[4,1152,256]{2,1,0:T(8,128)(2,1)} %all-gather.10.cloned.1.call-done, bf16[576,1152]{1,0:T(8,128)(2,1)} %param.23, bf16[1,576,4,256]{3,1,2,0:T(8,128)(2,1)S(1)} %copy-done.2), kind=kOutput, calls=%fused_computation.45 | convolution fusion | flops 1360723968 | bytes 6045696 | tf_op jit(solution)/shard_map/oc,fcp->fop/dot_general | solution.py:31
  314.1 32.8 %all_to_all.37 = bf16[4,576,256]{2,1,0:T(8,128)(2,1)S(1)} all-to-all(bf16[4,576,256]{2,1,0:T(8,128)(2,1)S(1)} %fusion.63), channel_id=1, replica_groups=mesh['groups'=2,'seq'=4,'heads'=2,'cfg'=2] {'seq'}, dimensions={0} | all-to-all | bytes 2359296 | tf_op jit(solution)/shard_map/all_to_all | solution.py:120
  346.8 0.1 copy.61
  347.0 0.1 collective-permute-start
  348.4 1.6 collective-permute-done
  350.0 2.2 fusion.91
  (17 shorter events, 0.2 us)
Async XLA Ops:
  6.5 130.9 %copy-start = (bf16[576,1152]{1,0:T(8,128)(2,1)S(1)}, bf16[576,1152]{1,0:T(8,128)(2,1)}, u32[]{:S(2)}) copy-start(bf16[576,1152]{1,0:T(8,128)(2,1)} %param.20) | copy-start | bytes 3981316
  6.5 41.1 %all-gather.12.cloned.1.call-start = ((), (), s32[]{:S(2)}) async-start(), calls=%async_computation.4 | async-start | bytes 3538944 | tf_op jit(solution)/shard_map/all_gather | solution.py:54
  7.3 130.2 %all-gather.8.cloned.1.call-start = ((), (), s32[]{:S(2)}) async-start(), calls=%async_computation.2 | async-start | bytes 3538944 | tf_op jit(solution)/shard_map/all_gather | solution.py:93
  47.7 2.4 copy-start.3
  101.3 131.0 %all-gather.14.cloned.1.call-start = ((), (), s32[]{:S(2)}) async-start(), calls=%async_computation.5 | async-start | bytes 3538944 | tf_op jit(solution)/shard_map/all_gather | solution.py:99
  196.5 1.8 copy-start.5
  198.0 112.3 %all-gather.10.cloned.1.call-start = ((), (), s32[]{:S(2)}) async-start(), calls=%async_computation.3 | async-start | bytes 3538944 | tf_op jit(solution)/shard_map/all_gather | solution.py:117
  232.3 2.4 copy-start.4
  259.4 2.2 copy-start.1
  269.9 40.4 %copy-start.2 = (bf16[1,576,4,256]{3,1,2,0:T(8,128)(2,1)S(1)}, bf16[1,576,4,256]{3,1,2,0:T(8,128)(2,1)}, u32[]{:S(2)}) copy-start(bf16[1,576,4,256]{3,1,2,0:T(8,128)(2,1)} %copy.46) | copy-start | bytes 3538948
  347.0 3.0 collective-permute-start
Sparse Core Ops, SparseCore 0:
  8.9 38.7 all-gather.11
  101.4 36.0 all-gather.7
  198.1 34.1 all-gather.13
  274.2 36.0 all-gather.9
where the time goes:
time: 364 us; the launch traced here: 359 us
  waiting for transfers between devices  137 us (38%)
  blocking collectives  73.5 us (20%)
  matrix products  70.3 us (19%)
  local copies, waits for them, and re-layouts  41.4 us (11%)
  other arithmetic  19.1 us (5%)
  between operations  15.5 us (4%)
    all_gather x1, waiting for transfers between devices, shards(): lax.all_gather(attended_time, 'heads', axis=1, tiled=True)  36.2 us
    all_gather x1, waiting for transfers between devices, shards(): lax.all_gather(attended, 'heads', axis=1, tiled=True)  36 us
    all_gather x1, waiting for transfers between devices, shards(): lax.all_gather(own_rows, 'heads', axis=1, tiled=True)  34.1 us
    all_to_all x1, blocking collectives, shards(): lax.all_to_all(after_spatial, 'seq', split_axis=2, concat_axis=0, tiled=T...  33 us
    all_to_all x1, blocking collectives, shards(): lax.all_to_all(block_out, 'seq', split_axis=0, concat_axis=2, tiled=True)  32.8 us
    all_gather x1, waiting for transfers between devices, shards(): video_piece = lax.all_gather(frame_tokens, 'heads', axis=1, tiled=True)  28.1 us
    dot_general x2, matrix products, block_step(): jnp.einsum('hpk,hek->hep', weights, value_rows[frame_id], preferred_eleme...  19.7 us
    unnamed x19, local copies, waits for them, and re-layouts  17.8 us
  transfers between devices with their start and end apart: 5, of which 5 were waited for; matrix products, arithmetic and copies ran while one was open for 1% of the time, Pallas kernels for 0%

commit v1 on v0

--- a/solution.py
+++ b/solution.py
@@ -92,7 +92,12 @@
     attended = jnp.transpose(attended, (0, 2, 3, 1, 4)).reshape(frame_count, width, positions)
     update = add_mixed(lax.all_gather(attended, "heads", axis=1, tiled=True), spatial_out)
     after_spatial = (frame_tokens.astype(jnp.float32) + update).astype(jnp.bfloat16)
-    own_rows = lax.all_to_all(after_spatial, "seq", split_axis=2, concat_axis=0, tiled=True)
+    own_rows = jnp.concatenate(
+        lax.all_to_all(
+            jnp.stack(jnp.split(after_spatial, lax.axis_size("seq"), axis=2)), "seq", 0, 0
+        ),
+        axis=0,
+    )
     frames_all = own_rows.shape[0]
     columns = own_rows.shape[2]
     piece_add, piece_sq = project_piece(

time: 364 us -> 335 us (0.920); the launches traced: 359 us -> 335 us
  local copies, waits for them, and re-layouts: 41.4 us -> 27.6 us
  other arithmetic: 19.1 us -> 9.33 us
    unnamed x1 -> x0, other arithmetic: 9.93 us -> none
    unnamed x19 -> x15, local copies, waits for them, and re-layouts: 17.8 us -> 9.5 us
    convert_element_type x1 -> x0, local copies, waits for them, and re-layouts: 4.11 us -> none  [shards(): (frame_tokens.astype(jnp.float32) + update).astype(jnp.bfloat16)]
where the time goes in v1:
time: 335 us
  waiting for transfers between devices  137 us (41%)
  blocking collectives  73.4 us (22%)
  matrix products  70.3 us (21%)
  local copies, waits for them, and re-layouts  27.6 us (8%)
  between operations  15.3 us (5%)
  other arithmetic  9.33 us (3%)
    all_gather x1, waiting for transfers between devices, shards(): lax.all_gather(attended_time, 'heads', axis=1, tiled=True)  36.2 us
    all_gather x1, waiting for transfers between devices, shards(): lax.all_gather(attended, 'heads', axis=1, tiled=True)  35.9 us
    all_gather x1, waiting for transfers between devices, shards(): lax.all_gather(own_rows, 'heads', axis=1, tiled=True)  34.3 us
    all_to_all x1, blocking collectives, shards(): lax.all_to_all(jnp.stack(jnp.split(after_spatial, lax.axis_size('seq'), a...  32.9 us
    all_to_all x1, blocking collectives, shards(): lax.all_to_all(block_out, 'seq', split_axis=0, concat_axis=2, tiled=True)  32.8 us
    all_gather x1, waiting for transfers between devices, shards(): video_piece = lax.all_gather(frame_tokens, 'heads', axis=1, tiled=True)  28.1 us
    dot_general x2, matrix products, block_step(): jnp.einsum('hpk,hek->hep', weights, value_rows[frame_id], preferred_eleme...  19.7 us
    dot_general x3, matrix products, project_piece(): jnp.einsum('kod,fdp->fkop', weight_piece, scaled, preferred_element_type=...  17.5 us
  transfers between devices with their start and end apart: 5, of which 5 were waited for; matrix products, arithmetic and copies ran while one was open for 1% of the time, Pallas kernels for 0%

profile of v1, /device:TPU:0, one launch (start us, length us, event | category | flops | bytes accessed | tf_op | source)
XLA Modules:
  0.0 334.6 jit_solution(12909776162323412480)
XLA Ops:
  6.5 0.0 copy-start
  6.5 0.0 all-gather.12.cloned.1.call-start
  6.5 0.7 all-gather.12.cloned.1.call-update
  7.3 0.0 all-gather.8.cloned.1.call-start
  7.3 0.7 convert_element_type.98
  8.7 7.7 %all-gather.1 = bf16[1,1,1152,128]{3,2,1,0:T(8,128)(2,1)S(1)} all-gather(bf16[1,1,576,128]{3,2,1,0:T(8,128)(2,1)} %param.14), channel_id=3, replica_groups=mesh['groups'=2,'seq'=4,'heads'=2,'cfg'=2] {'heads'}, dimensions={2}, use_global_device_ids=true | all-gather | bytes 442368 | tf_op jit(solution)/shard_map/all_gather | solution.py:55
  16.4 0.2 fusion.93
  16.6 3.0 fusion.87
  19.6 28.1 %all-gather.12.cloned.1.call-done = bf16[1,1,1152,1024]{3,2,1,0:T(8,128)(2,1)} async-done(((bf16[1,1,576,1024]{3,2,1,0:T(8,128)(2,1)}), bf16[1,1,1152,1024]{3,2,1,0:T(8,128)(2,1)}) %all-gather.12.cloned.1.call-update) | async-done | bytes 2359312 | tf_op jit(solution)/shard_map/all_gather | solution.py:54
  47.7 0.0 copy-start.3
  47.7 2.3 fusion.50
  50.0 0.0 copy-done.3
  50.1 7.3 %fusion.48 = bf16[1,1024,3,576]{1,3,2,0:T(8,128)(2,1)S(1)} fusion(f32[1024]{0:T(1024)S(1)} %add_rsqrt_fusion.1, bf16[3,576,1152]{2,1,0:T(8,128)(2,1)} %param.19, bf16[1,1,1152,1024]{3,2,1,0:T(8,128)(2,1)S(1)} %copy-done.3, f32[1152]{0:T(1024)S(1)} %convert_element_type.98), kind=kOutput, calls=%fused_computation.28 | convolution fusion | flops 4083941376 | bytes 9888256 | tf_op jit(solution)/shard_map/kod,fdp->fkop/dot_general | solution.py:26
  57.3 1.4 slice_bitcast_fusion
  58.7 1.3 pad_maximum_fusion
  60.1 36.6 %while.10 = (s32[]{:T(128)}, bf16[2,8,72,512]{3,2,1,0:T(8,128)(2,1)}, pred[1,1152]{1,0:T(4,128)(4,1)S(1)}, s32[2]{0:T(128)S(1)}, bf16[1,8,72,1024]{3,2,1,0:T(8,1...) while((s32[]{:T(128)}, ...), condition=%wide.region_5.6_spmd, body=%wide.region_2.5_spmd.sunk | while | flops 2081200384 | bytes 5788856 | solution.py:90
  60.1 0.7 dynamic_slice.50
  61.5 7.0 %exponential_reduce_fusion.2 = f32[8,512]{1,0:T(8,128)S(1)} fusion(pred[1152]{0:T(1024)(128)(4,1)S(1)} %reduce.4, bf16[1,8,72,1152]{3,2,1,0:T(8,128)(2,1)S(1)} %get-tuple-element.143, bf16[1,8,72,1024]{3,2,1,0:T(8,128)(2,1)} %get-tuple-element.142, s32[]{:T(128)S(6)} %select_n.52), kind=kOutput, calls=%fused_computation.5.clone.1 | convolution fusion | flops 698352768 | bytes 1934468 | tf_op jit(solution)/shard_map/while/body/eval_jaxpr/sub | solution.py:17
  68.5 9.8 %fusion.120 = bf16[2,8,72,512]{3,2,1,0:T(8,128)(2,1)} fusion(bf16[2,8,72,512]{3,2,1,0:T(8,128)(2,1)} %get-tuple-element.127, s32[]{:T(128)} %get-tuple-element.126, bf16[1,8,72,1152]{3,2,1,0:T(8,128)(2,1)} %get-tuple-element.144, f32[8,512]{1,0:T(8,128)S(1)} %exponential_reduce_fusion.2, pred[1152]{0:T(1024)(128)(4,1)S(1)} %reduce.4, ...), kind=kOutput, calls=%fused_computation.13.clone.1 | convolution fusion | flops 1382847616 | bytes 3851908 | tf_op jit(solution)/shard_map/while/body/eval_jaxpr/hpk,hek->hep/dot_general | solution.py:85
  78.4 0.7 dynamic_slice.50
  79.8 7.0 %exponential_reduce_fusion.2 = f32[8,512]{1,0:T(8,128)S(1)} fusion(pred[1152]{0:T(1024)(128)(4,1)S(1)} %reduce.4, bf16[1,8,72,1152]{3,2,1,0:T(8,128)(2,1)S(1)} %get-tuple-element.143, bf16[1,8,72,1024]{3,2,1,0:T(8,128)(2,1)} %get-tuple-element.142, s32[]{:T(128)S(6)} %select_n.52), kind=kOutput, calls=%fused_computation.5.clone.1 | convolution fusion | flops 698352768 | bytes 1934468 | tf_op jit(solution)/shard_map/while/body/eval_jaxpr/sub | solution.py:17
  86.8 9.8 %fusion.120 = bf16[2,8,72,512]{3,2,1,0:T(8,128)(2,1)} fusion(bf16[2,8,72,512]{3,2,1,0:T(8,128)(2,1)} %get-tuple-element.127, s32[]{:T(128)} %get-tuple-element.126, bf16[1,8,72,1152]{3,2,1,0:T(8,128)(2,1)} %get-tuple-element.144, f32[8,512]{1,0:T(8,128)S(1)} %exponential_reduce_fusion.2, pred[1152]{0:T(1024)(128)(4,1)S(1)} %reduce.4, ...), kind=kOutput, calls=%fused_computation.13.clone.1 | convolution fusion | flops 1382847616 | bytes 3851908 | tf_op jit(solution)/shard_map/while/body/eval_jaxpr/hpk,hek->hep/dot_general | solution.py:85
  96.6 2.5 copy.23
  99.1 1.7 reshape.108
  100.8 0.0 all-gather.8.cloned.1.call-update
  100.8 0.3 all-gather.14.cloned.1.call-start
  101.1 35.9 %all-gather.8.cloned.1.call-done = bf16[1,1152,1024]{2,1,0:T(8,128)(2,1)} async-done(((bf16[1,576,1024]{2,1,0:T(8,128)(2,1)}), bf16[1,1152,1024]{2,1,0:T(8,128)(2,1)}) %all-gather.8.cloned.1.call-update) | async-done | bytes 2359312 | tf_op jit(solution)/shard_map/all_gather | solution.py:93
  137.0 0.0 copy-done
  137.0 3.7 %fusion.64 = bf16[1,576,1024]{2,1,0:T(8,128)(2,1)S(1)} fusion(bf16[576,1152]{1,0:T(8,128)(2,1)S(1)} %copy-done, bf16[1,1152,1024]{2,1,0:T(8,128)(2,1)} %all-gather.8.cloned.1.call-done, bf16[1,1,576,1024]{3,2,1,0:T(8,128)(2,1)} %param.13), kind=kOutput, calls=%fused_computation.47 | convolution fusion | flops 1360723968 | bytes 6045696 | tf_op jit(solution)/shard_map/oc,fcp->fop/dot_general | solution.py:31
  140.7 0.1 slice_bitcast_fusion.6
  140.8 0.2 pad_maximum_fusion.2
  140.9 0.0 copy-start.5
  140.9 32.9 %all_to_all.23 = bf16[4,1,576,256]{3,2,1,0:T(8,128)(2,1)} all-to-all(bf16[4,1,576,256]{3,2,1,0:T(8,128)(2,1)S(1)} %pad_maximum_fusion.2), channel_id=1, replica_groups=mesh['groups'=2,'seq'=4,'heads'=2,'cfg'=2] {'seq'}, dimensions={0} | all-to-all | bytes 2359296 | tf_op jit(solution)/shard_map/all_to_all | solution.py:96
  173.8 0.0 all-gather.14.cloned.1.call-update
  173.8 0.0 all-gather.10.cloned.1.call-start
  173.9 0.0 copy-done.5
  173.9 34.3 %all-gather.14.cloned.1.call-done = bf16[4,1,1152,256]{3,2,1,0:T(8,128)(2,1)} async-done(((bf16[4,1,576,256]{3,2,1,0:T(8,128)(2,1)}), bf16[4,1,1152,256]{3,2,1,0:T(8,128)(2,1)}) %all-gather.14.cloned.1.call-update) | async-done | bytes 2359312 | tf_op jit(solution)/shard_map/all_gather | solution.py:104
  208.2 0.0 copy-start.4
  208.2 2.3 fusion.52
  210.5 0.1 copy-done.4
  210.6 7.2 %multiply_convert_fusion = bf16[4,256,3,576]{1,3,2,0:T(8,128)(2,1)S(1)} fusion(f32[4,256]{1,0:T(4,128)S(1)} %add_rsqrt_fusion, bf16[3,576,1152]{2,1,0:T(8,128)(2,1)} %param.22, bf16[4,1,1152,256]{3,2,1,0:T(8,128)(2,1)S(1)} %copy-done.4, f32[1152]{0:T(1024)S(1)} %convert_element_type.109), kind=kOutput, calls=%fused_computation.29 | convolution fusion | flops 4083941376 | bytes 9888256 | tf_op jit(solution)/shard_map/kod,fdp->fkop/dot_general | solution.py:26
  217.8 1.9 fusion.104
  219.7 2.8 copy.33
  222.5 4.1 %copy.34 = bf16[4,1,8,72,256]{3,0,4,2,1:T(4,128)(2,1)} copy(bf16[4,1,8,72,256]{4,3,2,1,0:T(8,128)(2,1)} %get-tuple-element.59) | data formatting | bytes 2359296
  226.6 5.8 %fusion.71 = f32[8,256,4,4]{3,2,1,0:T(4,128)} fusion(bf16[4,1,8,72,256]{3,0,4,2,1:T(4,128)(2,1)} %copy.34, bf16[4,1,8,72,256]{3,0,4,2,1:T(4,128)(2,1)S(1)} %copy.33), kind=kOutput, calls=%fused_computation.54 | convolution fusion | flops 4718592 | bytes 2490368 | tf_op jit(solution)/shard_map/fhep,ghep->hfgp/dot_general | solution.py:113
  232.4 2.8 copy.27
  235.3 0.0 copy-start.1
  235.4 2.1 copy.28
  237.5 0.0 copy-done.1
  237.5 2.5 copy.32
  240.0 5.8 %convert_bitcast_fusion = bf16[4,8,72,256]{2,0,3,1:T(4,128)(2,1)} fusion(bf16[8,4,4,256]{2,1,3,0:T(4,128)(2,1)} %copy.28, bf16[4,1,8,72,256]{3,0,4,2,1:T(4,128)(2,1)} %copy.32), kind=kOutput, calls=%fused_computation.59 | convolution fusion | flops 5308416 | bytes 2424832 | tf_op jit(solution)/shard_map/hfgp,ghep->fhep/dot_general | solution.py:117
  245.8 0.0 copy-start.2
  245.8 4.2 %copy.29 = bf16[4,8,72,256]{3,2,1,0:T(8,128)(2,1)} copy(bf16[4,8,72,256]{2,0,3,1:T(4,128)(2,1)} %convert_bitcast_fusion) | data formatting | bytes 2359296 | tf_op jit(solution)/shard_map/convert_element_type | solution.py:120
  250.0 0.0 all-gather.10.cloned.1.call-update
  250.0 36.2 %all-gather.10.cloned.1.call-done = bf16[4,1152,256]{2,1,0:T(8,128)(2,1)} async-done(((bf16[4,576,256]{2,1,0:T(8,128)(2,1)}), bf16[4,1152,256]{2,1,0:T(8,128)(2,1)}) %all-gather.10.cloned.1.call-update) | async-done | bytes 2359312 | tf_op jit(solution)/shard_map/all_gather | solution.py:122
  286.2 0.0 copy-done.2
  286.2 3.8 %fusion.63 = bf16[4,576,256]{2,1,0:T(8,128)(2,1)S(1)} fusion(bf16[4,1152,256]{2,1,0:T(8,128)(2,1)} %all-gather.10.cloned.1.call-done, bf16[576,1152]{1,0:T(8,128)(2,1)} %param.23, bf16[4,1,576,256]{3,2,1,0:T(8,128)(2,1)S(1)} %copy-done.2), kind=kOutput, calls=%fused_computation.45 | convolution fusion | flops 1360723968 | bytes 6045696 | tf_op jit(solution)/shard_map/oc,fcp->fop/dot_general | solution.py:31
  290.0 32.8 %all_to_all.24 = bf16[4,576,256]{2,1,0:T(8,128)(2,1)S(1)} all-to-all(bf16[4,576,256]{2,1,0:T(8,128)(2,1)S(1)} %fusion.63), channel_id=1, replica_groups=mesh['groups'=2,'seq'=4,'heads'=2,'cfg'=2] {'seq'}, dimensions={0} | all-to-all | bytes 2359296 | tf_op jit(solution)/shard_map/all_to_all | solution.py:125
  322.7 0.1 copy.35
  322.9 0.1 collective-permute-start
  324.3 1.6 collective-permute-done
  325.9 2.2 fusion.91
  (14 shorter events, 0.2 us)
Async XLA Ops:
  6.5 130.5 %copy-start = (bf16[576,1152]{1,0:T(8,128)(2,1)S(1)}, bf16[576,1152]{1,0:T(8,128)(2,1)}, u32[]{:S(2)}) copy-start(bf16[576,1152]{1,0:T(8,128)(2,1)} %param.20) | copy-start | bytes 3981316
  6.5 41.1 %all-gather.12.cloned.1.call-start = ((), (), s32[]{:S(2)}) async-start(), calls=%async_computation.4 | async-start | bytes 3538944 | tf_op jit(solution)/shard_map/all_gather | solution.py:54
  7.3 129.8 %all-gather.8.cloned.1.call-start = ((), (), s32[]{:S(2)}) async-start(), calls=%async_computation.2 | async-start | bytes 3538944 | tf_op jit(solution)/shard_map/all_gather | solution.py:93
  47.7 2.4 copy-start.3
  100.8 107.4 %all-gather.14.cloned.1.call-start = ((), (), s32[]{:S(2)}) async-start(), calls=%async_computation.5 | async-start | bytes 3538944 | tf_op jit(solution)/shard_map/all_gather | solution.py:104
  140.9 33.0 %copy-start.5 = (bf16[1152]{0:T(1024)(128)(2,1)S(1)}, bf16[1152]{0:T(1024)(128)(2,1)}, u32[]{:S(2)}) copy-start(bf16[1152]{0:T(1024)(128)(2,1)} %param.21) | copy-start | bytes 6916
  173.8 112.3 %all-gather.10.cloned.1.call-start = ((), (), s32[]{:S(2)}) async-start(), calls=%async_computation.3 | async-start | bytes 3538944 | tf_op jit(solution)/shard_map/all_gather | solution.py:122
  208.2 2.4 copy-start.4
  235.3 2.2 copy-start.1
  245.8 40.4 %copy-start.2 = (bf16[4,1,576,256]{3,2,1,0:T(8,128)(2,1)S(1)}, bf16[4,1,576,256]{3,2,1,0:T(8,128)(2,1)}, u32[]{:S(2)}) copy-start(bf16[4,1,576,256]{3,2,1,0:T(8,128)(2,1)} %all_to_all.23) | copy-start | bytes 3538948
  322.9 3.0 collective-permute-start
Sparse Core Ops, SparseCore 0:
  8.9 38.7 all-gather.11
  100.9 36.0 all-gather.7
  174.0 34.1 all-gather.13
  250.1 36.0 all-gather.9
